TPU v7x, 256 devices: a whole 4x4x8 slice. The times are simulated.
256 devices in a mesh: pb: 16 (over z, core), sp: 16 (over y, x).
Axes of the slice: x: 4, y: 4, z: 8, core: 2. Of those that a mesh axis runs over, the one named last changes fastest.
Arguments:
- nodes: bfloat16 [65536, 1024], P(('pb', 'sp')), may hold values from -40 to 40
- project_in: bfloat16 [1024, 3072], replicated, may hold values from -0.3 to 0.3
- project_out: bfloat16 [1024, 1024], replicated, may hold values from -0.1875 to 0.1875
- tile_list: int32 [512, 32], replicated, may hold values from 0 to 511, as said below
- tile_count: int32 [512], replicated, may hold values from 2 to 32, as said below
Outputs:
- mixed: bfloat16 [65536, 1024], P(('pb', 'sp'))
Inputs may be any that keep to these rules, and one draw needn't show every extreme that they name: `tile_list`: position 0 of row t is t itself. Over the live positions of the rows of one group (rows g * 32 to (g + 1) * 32 - 1), at most 4 distinct tiles of any other group are listed, and exactly 4 of the next group's tiles (group g + 1, after the last comes the first). A tile may stand more than once in a row. `tile_count`: row 0 has 32.
All inputs are finite; a program needn't handle non-finite values.
Results may differ from a plain program's by a relative error of at most 0.0082.
Values may be sent and summed in bfloat16 or wider, within the bound.
A program may use at most 128 MiB of HBM per device.

v0:
```python
import functools

import jax
import jax.numpy as jnp
from jax import lax
from jax.experimental import pallas as pl
from jax.experimental.pallas import tpu as pltpu
from jax.sharding import PartitionSpec as P

D = 1024
HEADS = 16
HEAD_DIM = 64
TILE = 128
LISTED = 32
SLOTS = 4
GROUP = 32
N = 16
CHUNK = 4
EARLY = 12
LOW = -1e30
MESH = pl.DeviceIdType.MESH


def build_tables(list_ref, count_ref, marked_ref, tab_ref, grp):
    f32, b16, i32 = jnp.float32, jnp.bfloat16, jnp.int32
    base = grp * GROUP
    places = lax.broadcasted_iota(i32, (LISTED, N * GROUP), 0)
    across = jnp.where(places < count_ref[...], list_ref[...], -1)
    for b in range(0, N * GROUP, TILE):
        marked_ref[b:b + TILE, :] = across[:, b:b + TILE].T
    lane = lax.broadcasted_iota(i32, (N, TILE), 1)

    def uses(i, used):
        hit = jnp.where(marked_ref[...] == base + i, 1.0, 0.0)
        hit = jnp.max(hit.reshape(N, GROUP, LISTED), axis=1)
        return jnp.where(lane == i, jnp.max(hit, axis=1, keepdims=True), used)

    used = lax.fori_loop(0, GROUP, uses, jnp.zeros((N, TILE), f32), unroll=4)
    low = lax.broadcasted_iota(i32, (TILE, TILE), 0) < lax.broadcasted_iota(i32, (TILE, TILE), 1)
    rank = jnp.dot(used.astype(b16), jnp.where(low, 1.0, 0.0).astype(b16), preferred_element_type=f32)
    send = jnp.zeros((N, TILE), f32)
    for k in range(SLOTS):
        pick = jnp.where((rank == k) & (used > 0), lane.astype(f32), 0.0)
        send = jnp.where(lane == k, jnp.sum(pick, axis=1, keepdims=True), send)
    tab_ref[GROUP:] = send.astype(i32)
    tiles = N * GROUP
    own = marked_ref[pl.ds(pl.multiple_of(base, GROUP), GROUP), :]
    tile = lax.broadcasted_iota(i32, (GROUP, tiles), 1)
    present = jnp.zeros((GROUP, tiles), f32)
    for j in range(LISTED):
        present = jnp.where(own[:, j:j + 1] == tile, 1.0, present)
    up = lax.broadcasted_iota(i32, (tiles, tiles), 0)
    across = lax.broadcasted_iota(i32, (tiles, tiles), 1)
    before = up < across
    same = before & (lax.div(up, GROUP) == lax.div(across, GROUP))
    before = jnp.where(before, 1.0, 0.0).astype(b16)
    same = jnp.where(same, 1.0, 0.0).astype(b16)
    wanted = jnp.broadcast_to(jnp.max(present, axis=0, keepdims=True), (N, tiles))
    rank = jnp.dot(wanted.astype(b16), same, preferred_element_type=f32)[0:1]
    owner = lax.div(tile, GROUP)
    here = owner == grp
    slot = jnp.where(here, (tile - base).astype(f32), (GROUP + SLOTS * owner).astype(f32) + rank)
    near = jnp.where(here, present, 0.0)
    away = jnp.where(here, 0.0, present)
    both = jnp.concatenate([near, away], axis=0).astype(b16)
    order = jnp.dot(both, before, preferred_element_type=f32)
    near_count = jnp.sum(near, axis=1, keepdims=True)
    count = jnp.sum(present, axis=1, keepdims=True)
    order = jnp.where(here, order[:GROUP], order[GROUP:] + near_count)
    order = jnp.where(present > 0, order, -1.0)
    wide = lax.broadcasted_iota(i32, (GROUP, TILE), 1)

    def place(k, out):
        v = jnp.sum(jnp.where(order == k.astype(f32), slot, 0.0), axis=1, keepdims=True)
        return jnp.where(wide == k, v, out)

    out = lax.fori_loop(0, LISTED, place, jnp.zeros((GROUP, TILE), f32), unroll=4)
    out = jnp.where(wide == LISTED, near_count, out)
    out = jnp.where(wide == LISTED + 1, count, out)
    tab_ref[:GROUP] = out.astype(i32)


def scratch_state():
    f32 = jnp.float32
    square = pltpu.VMEM((TILE, TILE), f32)
    return [
        pltpu.VMEM((2, TILE, CHUNK * TILE), f32),
        pltpu.VMEM((TILE, CHUNK * TILE), jnp.bfloat16),
        square, square, square, square,
    ]


def clear_stages(s_buf, p_buf, m_cur, m_max, a_cur, a_old):
    for ref in (s_buf, p_buf, m_cur, m_max, a_cur, a_old):
        ref[...] = jnp.zeros_like(ref)


def run_stages(slot, items, fetch, live, qz, state, buffers):
    acc, total, top = state
    s_buf, p_buf, m_cur, m_max, a_cur, a_old = buffers
    (r0, c0), (r1, _), (r2, _), (r3, c3) = items
    added = jnp.dot(p_buf[...], fetch(r3, c3), preferred_element_type=jnp.float32)
    acc[r3] = acc[r3] * a_old[...] + added
    m = m_cur[...]
    fade = a_cur[...]
    part = None
    for t in range(CHUNK):
        cols = slice(t * TILE, (t + 1) * TILE)
        w = jnp.exp(s_buf[slot, :, cols] - m)
        p_buf[:, cols] = w.astype(jnp.bfloat16)
        part = w if part is None else part + w
    total[r2] = total[r2] * fade + part
    a_old[...] = fade
    before = top[r1]
    now = jnp.maximum(before, jnp.max(m_max[...], axis=1, keepdims=True))
    top[r1] = now
    m_cur[...] = now
    a_cur[...] = jnp.exp(before - now)
    row = jnp.minimum(r0, GROUP - 1)
    s = lax.dot_general(
        qz[row], fetch(r0, c0), (((1,), (1,)), ((), ())), preferred_element_type=jnp.float32)
    big = None
    for t in range(CHUNK):
        cols = slice(t * TILE, (t + 1) * TILE)
        st = s[:, cols] + jnp.where(c0 + t < live(row), 0.0, LOW)
        s_buf[slot, :, cols] = st
        big = st if big is None else jnp.maximum(big, st)
    m_max[...] = big


def exchange_kernel(
    list_hbm, count_hbm, nodes_hbm, w_hbm, qz, kv_out, far_out, tab_out, acc, total, top,
    w_buf, kv_send, q_send, q_got, far_send, list_ref, count_ref, nodes_ref, marked, tab, in_sem, w_sem, kv_ss, kv_rs, q_ss, q_rs, z_ss, z_rs, t_sem,
    *buffers,
):
    me = lax.axis_index("sp")
    grp = lax.axis_index("pb")

    def w_copy(p):
        cols = pl.ds(pl.multiple_of(p * 384, 128), 384)
        return pltpu.make_async_copy(w_hbm.at[:, cols], w_buf.at[p], w_sem.at[p])

    def pair(i):
        return lax.rem(me // 2 + i, 8)

    arrivals = [
        pltpu.make_async_copy(a, b, in_sem.at[i])
        for i, (a, b) in enumerate(((nodes_hbm, nodes_ref), (list_hbm, list_ref), (count_hbm, count_ref)))
    ]
    for copy in arrivals:
        copy.start()
    for i in range(8):
        w_copy(pair(i)).start()

    barrier = pltpu.get_barrier_semaphore()

    def greet(d, _):
        pl.semaphore_signal(barrier, inc=1, device_id={"sp": lax.rem(me + d, N)}, device_id_type=MESH)
        pl.semaphore_signal(barrier, inc=1, device_id={"pb": lax.rem(grp + d, N)}, device_id_type=MESH)
        return 0

    lax.fori_loop(1, N, greet, 0)
    pl.semaphore_wait(barrier, 2 * (N - 1))

    def kv_copy(src, dst, idx):
        return pltpu.make_async_remote_copy(
            src_ref=kv_send.at[dst], dst_ref=kv_out.at[pl.ds(2 * idx, 2)], send_sem=kv_ss.at[dst],
            recv_sem=kv_rs.at[idx], device_id={"sp": dst}, device_id_type=MESH)

    def q_copy(dst, idx):
        return pltpu.make_async_remote_copy(
            src_ref=q_send.at[dst], dst_ref=q_got.at[idx], send_sem=q_ss.at[dst],
            recv_sem=q_rs.at[idx], device_id={"sp": dst}, device_id_type=MESH)

    def project(i, _):
        p = pair(i)
        w_copy(p).wait()
        y = jnp.dot(nodes_ref[...], w_buf[p], preferred_element_type=jnp.float32)
        for k in range(2):
            h = 2 * p + k
            o = k * 192
            q = (y[:, o:o + 64] * HEAD_DIM ** -0.5).astype(jnp.bfloat16)
            kv_send[h] = y[:, o + 64:o + 192].astype(jnp.bfloat16).reshape(2, TILE, TILE)
            q_send[h] = jnp.concatenate([q[:TILE], q[TILE:]], axis=1)

            @pl.when(h != me)
            def _():
                kv_copy(me, h, me).start()
        return 0

    for copy in arrivals:
        copy.wait()
    lax.fori_loop(0, 8, project, 0)
    kv_out[pl.ds(2 * me, 2)] = kv_send[me]
    q_got[me] = q_send[me]

    def send_q(d, _):
        q_copy(lax.rem(me + d, N), me).start()
        return 0

    lax.fori_loop(1, N, send_q, 0)

    build_tables(list_ref, count_ref, marked, tab_out, grp)
    to_scalar = pltpu.make_async_copy(tab_out, tab, t_sem)
    to_scalar.start()

    def clear(r, _):
        acc[r] = jnp.zeros((TILE, TILE), jnp.float32)
        total[r] = jnp.zeros((TILE, TILE), jnp.float32)
        top[r] = jnp.full((TILE, TILE), LOW, jnp.float32)
        return 0

    lax.fori_loop(0, GROUP + 1, clear, 0)
    clear_stages(*buffers)
    to_scalar.wait()

    def wait_kv(d, _):
        s = lax.rem(me + N - d, N)
        kv_copy(me, s, s).wait_recv()
        return 0

    lax.fori_loop(1, N, wait_kv, 0)

    def far_copy(dst, idx):
        return pltpu.make_async_remote_copy(
            src_ref=far_send.at[dst], dst_ref=far_out.at[pl.ds(SLOTS * idx, SLOTS)], send_sem=z_ss.at[dst],
            recv_sem=z_rs.at[idx], device_id={"pb": dst}, device_id_type=MESH)

    def select(d, _):
        half = lax.div(d + 1, 2)
        off = 8 + half * (2 * lax.rem(d, 2) - 1)
        dst = lax.rem(grp + off, N)
        for k in range(SLOTS):
            far_send[dst, k] = kv_out[jnp.clip(tab[GROUP + dst, k], 0, GROUP - 1)]
        far_copy(dst, grp).start()
        return 0

    lax.fori_loop(0, N - 1, select, 0)
    far_out[pl.ds(SLOTS * grp, SLOTS)] = kv_out[0:SLOTS]

    def drain(d, _):
        s = lax.rem(me + N - d, N)
        q_copy(s, s).wait_recv()
        q_copy(s, s).wait_send()
        kv_copy(me, s, s).wait_send()
        return 0

    lax.fori_loop(1, N, drain, 0)
    zero64 = jnp.zeros((TILE, HEAD_DIM), jnp.bfloat16)

    def setup(s, _):
        both = q_got[s]
        qz[2 * s] = jnp.concatenate([both[:, :HEAD_DIM], zero64], axis=1)
        qz[2 * s + 1] = jnp.concatenate([both[:, HEAD_DIM:], zero64], axis=1)
        return 0

    lax.fori_loop(0, N, setup, 0)

    def fetch(r, c):
        row = jnp.minimum(r, GROUP - 1)
        return jnp.concatenate(
            [kv_out[jnp.clip(tab[row, c + t], 0, GROUP - 1)] for t in range(CHUNK)], axis=0)

    per_row = EARLY // CHUNK
    steps = GROUP * per_row

    def item(i):
        valid = (i >= 0) & (i < steps)
        i = jnp.clip(i, 0, steps - 1)
        row = lax.div(i, per_row)
        return jnp.where(valid, row, GROUP), (i - row * per_row) * CHUNK

    def advance(i, _):
        run_stages(
            lax.rem(i, 2), [item(i - k) for k in range(4)], fetch,
            lambda row: tab[row, LISTED], qz, (acc, total, top), buffers)
        return 0

    lax.fori_loop(0, steps + 3, advance, 0)

    def drain_far(d, _):
        s = lax.rem(grp + N - d, N)
        far_copy(s, s).wait_recv()
        far_copy(s, s).wait_send()
        return 0

    lax.fori_loop(1, N, drain_far, 0)


def exchange(listed, count, nodes, project_in):
    b16, f32, i32 = jnp.bfloat16, jnp.float32, jnp.int32
    vm = pl.BlockSpec(memory_space=pltpu.VMEM)
    dma = pltpu.SemaphoreType.DMA
    state = jax.ShapeDtypeStruct((GROUP + 1, TILE, TILE), f32)
    return pl.pallas_call(
        exchange_kernel,
        out_shape=(
            jax.ShapeDtypeStruct((GROUP, TILE, TILE), b16),
            jax.ShapeDtypeStruct((GROUP, TILE, TILE), b16),
            jax.ShapeDtypeStruct((N * SLOTS, TILE, TILE), b16),
            jax.ShapeDtypeStruct((GROUP + N, TILE), i32),
            state, state, state,
        ),
        in_specs=[pl.BlockSpec(memory_space=pltpu.HBM)] * 4,
        out_specs=(vm,) * 7,
        scratch_shapes=[
            pltpu.VMEM((8, D, 384), b16),
            pltpu.VMEM((N, 2, TILE, TILE), b16),
            pltpu.VMEM((N, TILE, TILE), b16),
            pltpu.VMEM((N, TILE, TILE), b16),
            pltpu.VMEM((N, SLOTS, TILE, TILE), b16),
            pltpu.VMEM((LISTED, N * GROUP), i32),
            pltpu.VMEM((1, N * GROUP), i32),
            pltpu.VMEM((2 * TILE, D), b16),
            pltpu.VMEM((N * GROUP, LISTED), i32),
            pltpu.SMEM((GROUP + N, TILE), i32),
            dma((3,)), dma((8,)), dma((N,)), dma((N,)), dma((N,)), dma((N,)), dma((N,)), dma((N,)), dma,
            *scratch_state(),
        ],
        compiler_params=pltpu.CompilerParams(
            collective_id=0, has_side_effects=True, vmem_limit_bytes=30 << 20),
        name="exchange",
    )(listed, count, nodes, project_in)


def attend_kernel(
    tab, qz, kv_ref, far_ref, acc_in, total_in, top_in, out_ref, acc, total, top, kv, rows, *buffers,
):
    kv[0:GROUP] = kv_ref[...]
    kv[GROUP:] = far_ref[...]
    lane = lax.broadcasted_iota(jnp.int32, (TILE, TILE), 1)
    clear_stages(*buffers)

    def first(r):
        return jnp.minimum(tab[r, LISTED], EARLY)

    def gather(r, carry):
        n, items = carry
        left = tab[r, LISTED + 1] - first(r)
        rows[n] = r
        return n + jnp.where(left > 0, 1, 0), items + lax.div(left + CHUNK - 1, CHUNK)

    used, items = lax.fori_loop(0, GROUP, gather, (jnp.int32(0), jnp.int32(0)))
    rows[used] = GROUP

    def fetch(r, c):
        row = jnp.minimum(r, GROUP - 1)
        return jnp.concatenate(
            [kv[tab[row, jnp.minimum(c + t, LISTED - 1)]] for t in range(CHUNK)], axis=0)

    def advance(i, state):
        n, r0, c0, r1, c1, r2, c2, r3, c3 = state
        run_stages(
            lax.rem(i, 2), ((r0, c0), (r1, c1), (r2, c2), (r3, c3)), fetch,
            lambda row: tab[row, LISTED + 1], qz, (acc, total, top), buffers)
        row = jnp.minimum(r0, GROUP - 1)
        more = (c0 + CHUNK < tab[row, LISTED + 1]) & (r0 < GROUP)
        n = jnp.where(more, n, jnp.minimum(n + 1, used))
        rn = jnp.where(more, r0, rows[n])
        cn = jnp.where(more, c0 + CHUNK, first(jnp.minimum(rn, GROUP - 1)))
        return n, rn, cn, r0, c0, r1, c1, r2, c2

    r = rows[0]
    zero, dummy = jnp.int32(0), jnp.int32(GROUP)
    start = (zero, r, first(jnp.minimum(r, GROUP - 1)), dummy, zero, dummy, zero, dummy, zero)
    lax.fori_loop(0, items + 3, advance, start)

    def finish(s, _):
        even = acc[2 * s] / jnp.sum(total[2 * s], axis=1, keepdims=True)
        odd = acc[2 * s + 1] / jnp.sum(total[2 * s + 1], axis=1, keepdims=True)
        even = pltpu.roll(even, HEAD_DIM, 1)
        out_ref[s] = jnp.where(lane < HEAD_DIM, even, odd).astype(jnp.bfloat16)
        return 0

    lax.fori_loop(0, N, finish, 0)


def attend(tab, qz, kv, far, acc, total, top):
    b16 = jnp.bfloat16
    vm = pl.BlockSpec(memory_space=pltpu.VMEM)
    state = jax.ShapeDtypeStruct(acc.shape, acc.dtype)
    return pl.pallas_call(
        attend_kernel,
        out_shape=(jax.ShapeDtypeStruct((N, TILE, TILE), b16), state, state, state),
        in_specs=[pl.BlockSpec(memory_space=pltpu.SMEM)] + [vm] * 6,
        out_specs=(vm,) * 4,
        input_output_aliases={4: 1, 5: 2, 6: 3},
        scratch_shapes=[
            pltpu.VMEM((GROUP + N * SLOTS, TILE, TILE), b16),
            pltpu.SMEM((GROUP + 1,), jnp.int32),
            *scratch_state(),
        ],
        compiler_params=pltpu.CompilerParams(vmem_limit_bytes=24 << 20),
        name="attend",
    )(tab, qz, kv, far, acc, total, top)[0]


def finish_kernel(att_ref, nodes_ref, w_ref, out_ref, got, joined, ss, rs):
    me = lax.axis_index("sp")
    barrier = pltpu.get_barrier_semaphore()

    def greet(d, _):
        pl.semaphore_signal(barrier, inc=1, device_id={"sp": lax.rem(me + d, N)}, device_id_type=MESH)
        return 0

    lax.fori_loop(1, N, greet, 0)
    pl.semaphore_wait(barrier, N - 1)

    def copy(dst, idx):
        return pltpu.make_async_remote_copy(
            src_ref=att_ref.at[dst], dst_ref=got.at[idx], send_sem=ss.at[dst],
            recv_sem=rs.at[idx], device_id={"sp": dst}, device_id_type=MESH)

    def send(d, _):
        copy(lax.rem(me + d, N), me).start()
        return 0

    lax.fori_loop(1, N, send, 0)
    got[me] = att_ref[me]

    def drain(d, _):
        s = lax.rem(me + N - d, N)
        copy(s, s).wait_recv()
        copy(s, s).wait_send()
        return 0

    lax.fori_loop(1, N, drain, 0)
    for p in range(HEADS // 2):
        a, b = got[2 * p], got[2 * p + 1]
        cols = slice(p * TILE, (p + 1) * TILE)
        joined[:TILE, cols] = jnp.concatenate([a[:, :HEAD_DIM], b[:, :HEAD_DIM]], axis=1)
        joined[TILE:, cols] = jnp.concatenate([a[:, HEAD_DIM:], b[:, HEAD_DIM:]], axis=1)
    for c in range(4):
        cols = slice(c * 256, (c + 1) * 256)
        y = jnp.dot(joined[...], w_ref[:, cols], preferred_element_type=jnp.float32)
        out_ref[:, cols] = (nodes_ref[:, cols].astype(jnp.float32) + y).astype(jnp.bfloat16)


def finish(att, nodes, project_out):
    b16 = jnp.bfloat16
    vm = pl.BlockSpec(memory_space=pltpu.VMEM)
    dma = pltpu.SemaphoreType.DMA
    return pl.pallas_call(
        finish_kernel,
        out_shape=jax.ShapeDtypeStruct((2 * TILE, D), b16),
        in_specs=[vm, vm, vm],
        out_specs=vm,
        scratch_shapes=[
            pltpu.VMEM((N, TILE, TILE), b16),
            pltpu.VMEM((2 * TILE, D), b16),
            dma((N,)), dma((N,)),
        ],
        compiler_params=pltpu.CompilerParams(
            collective_id=1, has_side_effects=True, vmem_limit_bytes=24 << 20),
        name="finish",
    )(att, nodes, project_out)


def shards(nodes, project_in, project_out, tile_list, tile_count):
    arguments = (tile_list.T, tile_count[None, :], nodes, project_in)
    arguments = [pltpu.with_memory_space_constraint(a, pltpu.HBM) for a in arguments]
    qz, kv, far, tab, acc, total, top = exchange(*arguments)
    att = attend(tab, qz, kv, far, acc, total, top)
    return finish(att, nodes, project_out)


def solution(mesh):
    in_specs = (P(("pb", "sp"), None), P(), P(), P(), P())
    out_specs = P(("pb", "sp"), None)
    return jax.shard_map(shards, mesh=mesh, in_specs=in_specs, out_specs=out_specs, check_vma=False)
```

profile of v0, /device:TPU:8, one launch (start us, length us, event | category | flops | bytes accessed | tf_op | source)
XLA Modules:
  0.0 103.4 jit_solution(6662341428060410017)
XLA Ops:
  0.0 72.8 %exchange.1 = (bf16[32,128,128]{2,1,0:T(8,128)(2,1)S(1)}, bf16[32,128,128]{2,1,0:T(8,128)(2,1)S(1)}, bf16[64,128,128]{2,1,0:T(8,128)(2,1)S(1)}, s32[48,128]{1,0:...) custom-call(s32[32,512]{1,0:T(8,128)} %bitcast.2, ...), custom_call_target="tpu_custom_call" | custom-call | tf_op jit(solution)/shard_map/exchange/pallas_call | solution.py:295
  72.8 0.0 copy-start
  72.8 0.0 copy-start.1
  72.8 17.1 %attend.1 = (bf16[16,128,128]{2,1,0:T(8,128)(2,1)S(1)}, f32[33,128,128]{2,1,0:T(8,128)S(1)}, f32[33,128,128]{2,1,0:T(8,128)S(1)}, f32[33,128,128]{2,1,0:T(8,128)S(1)}) custom-call(s32[48,128]{1,0:T(8,128)S(1)} %get-tuple-element.13.tab, bf16[32,128,128]{2,1,0:T(8,128)(2,1)S(1)} %get-tuple-element.14.qz, ...), custom_call_target="tpu_custom_call", output_to_operand_aliasing={{1}: (4, {}), {2}: (5, {}), {3}: (6, {})} | custom-call | tf_op jit(solution)/shard_map/attend/pallas_call | solution.py:382
  89.9 0.0 copy-done
  89.9 0.0 copy-done.1
  89.9 12.7 %finish.1 = bf16[256,1024]{1,0:T(8,128)(2,1)S(1)} custom-call(bf16[16,128,128]{2,1,0:T(8,128)(2,1)S(1)} %get-tuple-element.20.att_ref, bf16[256,1024]{1,0:T(8,128)(2,1)S(1)} %copy-done, bf16[1024,1024]{1,0:T(8,128)(2,1)S(1)} %copy-done.1), custom_call_target="tpu_custom_call" | custom-call | tf_op jit(solution)/shard_map/finish/pallas_call | solution.py:443
  102.6 0.8 copy.13
Async XLA Ops:
  72.8 17.1 %copy-start = (bf16[256,1024]{1,0:T(8,128)(2,1)S(1)}, bf16[256,1024]{1,0:T(8,128)(2,1)}, u32[]{:S(2)}) copy-start(bf16[256,1024]{1,0:T(8,128)(2,1)} %nodes_ref.1) | copy-start | bytes 1572868
  72.8 17.1 %copy-start.1 = (bf16[1024,1024]{1,0:T(8,128)(2,1)S(1)}, bf16[1024,1024]{1,0:T(8,128)(2,1)}, u32[]{:S(2)}) copy-start(bf16[1024,1024]{1,0:T(8,128)(2,1)} %w_ref.1) | copy-start | bytes 6291460
where the time goes:
time: 103 us
  Pallas kernels  103 us (100%)
    pallas_call x1, Pallas kernels, exchange(): pl.pallas_call(exchange_kernel, out_shape=(jax.ShapeDtypeStruct((GROUP, T...  72.8 us
    pallas_call x1, Pallas kernels, attend(): pl.pallas_call(attend_kernel, out_shape=(jax.ShapeDtypeStruct((N, TILE, T...  17.1 us
    pallas_call x1, Pallas kernels, finish(): pl.pallas_call(finish_kernel, out_shape=jax.ShapeDtypeStruct((2 * TILE, D...  12.7 us

commit v1 on v0

--- a/solution.py
+++ b/solution.py
@@ -16,7 +16,10 @@
 GROUP = 32
 N = 16
 CHUNK = 4
-EARLY = 12
+EARLY = 8
+HALF = GROUP // 2
+RAW = 2
+PART = TILE // N
 LOW = -1e30
 MESH = pl.DeviceIdType.MESH
 
@@ -59,7 +62,9 @@
     rank = jnp.dot(wanted.astype(b16), same, preferred_element_type=f32)[0:1]
     owner = lax.div(tile, GROUP)
     here = owner == grp
-    slot = jnp.where(here, (tile - base).astype(f32), (GROUP + SLOTS * owner).astype(f32) + rank)
+    raw = (GROUP + RAW * owner).astype(f32) + rank
+    cooked = (GROUP + RAW * N - RAW + (SLOTS - RAW) * owner).astype(f32) + rank
+    slot = jnp.where(here, (tile - base).astype(f32), jnp.where(rank < RAW, raw, cooked))
     near = jnp.where(here, present, 0.0)
     away = jnp.where(here, 0.0, present)
     both = jnp.concatenate([near, away], axis=0).astype(b16)
@@ -83,19 +88,19 @@
 def scratch_state():
     f32 = jnp.float32
     square = pltpu.VMEM((TILE, TILE), f32)
-    return [
+    return 2 * [
         pltpu.VMEM((2, TILE, CHUNK * TILE), f32),
         pltpu.VMEM((TILE, CHUNK * TILE), jnp.bfloat16),
         square, square, square, square,
     ]
 
 
-def clear_stages(s_buf, p_buf, m_cur, m_max, a_cur, a_old):
-    for ref in (s_buf, p_buf, m_cur, m_max, a_cur, a_old):
+def clear_stages(buffers):
+    for ref in buffers:
         ref[...] = jnp.zeros_like(ref)
 
 
-def run_stages(slot, items, fetch, live, qz, state, buffers):
+def run_stages(slot, items, fetch, live, qz, base, state, buffers):
     acc, total, top = state
     s_buf, p_buf, m_cur, m_max, a_cur, a_old = buffers
     (r0, c0), (r1, _), (r2, _), (r3, c3) = items
@@ -116,7 +121,7 @@
     top[r1] = now
     m_cur[...] = now
     a_cur[...] = jnp.exp(before - now)
-    row = jnp.minimum(r0, GROUP - 1)
+    row = jnp.minimum(r0, HALF - 1) + base
     s = lax.dot_general(
         qz[row], fetch(r0, c0), (((1,), (1,)), ((), ())), preferred_element_type=jnp.float32)
     big = None
@@ -129,8 +134,11 @@
 
 
 def exchange_kernel(
-    list_hbm, count_hbm, nodes_hbm, w_hbm, qz, kv_out, far_out, tab_out, acc, total, top,
-    w_buf, kv_send, q_send, q_got, far_send, list_ref, count_ref, nodes_ref, marked, tab, in_sem, w_sem, kv_ss, kv_rs, q_ss, q_rs, z_ss, z_rs, t_sem,
+    list_hbm, count_hbm, nodes_hbm, parts_hbm, w_hbm,
+    qz, kv_out, raw_out, far_out, tab_out, acc_a, total_a, top_a, acc_b, total_b, top_b,
+    w_buf, kv_send, q_send, q_got, far_send, parts, part_got, part_send, part_far, raw_send, raw_got,
+    list_ref, count_ref, nodes_ref, marked, tab, in_sem, w_sem, kv_ss, kv_rs, q_ss, q_rs, z_ss, z_rs,
+    p_ss, p_rs, y_ss, y_rs, r_ss, r_rs, t_sem,
     *buffers,
 ):
     me = lax.axis_index("sp")
@@ -145,7 +153,8 @@
 
     arrivals = [
         pltpu.make_async_copy(a, b, in_sem.at[i])
-        for i, (a, b) in enumerate(((nodes_hbm, nodes_ref), (list_hbm, list_ref), (count_hbm, count_ref)))
+        for i, (a, b) in enumerate((
+            (parts_hbm, parts), (nodes_hbm, nodes_ref), (list_hbm, list_ref), (count_hbm, count_ref)))
     ]
     for copy in arrivals:
         copy.start()
@@ -188,9 +197,23 @@
                 kv_copy(me, h, me).start()
         return 0
 
-    for copy in arrivals:
+    def part_copy(dst, idx):
+        return pltpu.make_async_remote_copy(
+            src_ref=parts.at[:, dst], dst_ref=part_got.at[pl.ds(2 * idx, 2)], send_sem=p_ss.at[dst],
+            recv_sem=p_rs.at[idx], device_id={"sp": dst}, device_id_type=MESH)
+
+    def send_part(d, _):
+        part_copy(lax.rem(me + d, N), me).start()
+        return 0
+
+    arrivals[0].wait()
+    lax.fori_loop(1, N, send_part, 0)
+    own_part = pltpu.make_async_copy(parts.at[:, me], part_got.at[pl.ds(2 * me, 2)], in_sem.at[0])
+    own_part.start()
+    for copy in arrivals[1:]:
         copy.wait()
     lax.fori_loop(0, 8, project, 0)
+    own_part.wait()
     kv_out[pl.ds(2 * me, 2)] = kv_send[me]
     q_got[me] = q_send[me]
 
@@ -204,15 +227,47 @@
     to_scalar = pltpu.make_async_copy(tab_out, tab, t_sem)
     to_scalar.start()
 
+    states = ((acc_a, total_a, top_a), (acc_b, total_b, top_b))
+
     def clear(r, _):
-        acc[r] = jnp.zeros((TILE, TILE), jnp.float32)
-        total[r] = jnp.zeros((TILE, TILE), jnp.float32)
-        top[r] = jnp.full((TILE, TILE), LOW, jnp.float32)
-        return 0
-
-    lax.fori_loop(0, GROUP + 1, clear, 0)
-    clear_stages(*buffers)
+        for acc, total, top in states:
+            acc[r] = jnp.zeros((TILE, TILE), jnp.float32)
+            total[r] = jnp.zeros((TILE, TILE), jnp.float32)
+            top[r] = jnp.full((TILE, TILE), LOW, jnp.float32)
+        return 0
+
+    lax.fori_loop(0, HALF + 1, clear, 0)
+    clear_stages(buffers)
     to_scalar.wait()
+
+    def off_of(d):
+        half = lax.div(d + 1, 2)
+        return 8 + half * (2 * lax.rem(d, 2) - 1)
+
+    def part_wait(d, _):
+        s = lax.rem(me + N - d, N)
+        part_copy(s, s).wait_recv()
+        return 0
+
+    lax.fori_loop(1, N, part_wait, 0)
+
+    def wanted(dst, k):
+        return jnp.clip(tab[GROUP + dst, k], 0, GROUP - 1)
+
+    def far_part(dst, idx):
+        return pltpu.make_async_remote_copy(
+            src_ref=part_send.at[dst], dst_ref=part_far.at[idx], send_sem=y_ss.at[dst],
+            recv_sem=y_rs.at[idx], device_id={"pb": dst}, device_id_type=MESH)
+
+    def select_part(d, _):
+        dst = lax.rem(grp + off_of(d), N)
+        rows = [part_got[wanted(dst, k)].astype(jnp.float32) for k in range(RAW)]
+        part_send[dst] = jnp.concatenate(rows, axis=0).astype(jnp.bfloat16)
+        far_part(dst, grp).start()
+        return 0
+
+    lax.fori_loop(0, N - 1, select_part, 0)
+    part_far[grp] = jnp.zeros((RAW * PART, D), jnp.bfloat16)
 
     def wait_kv(d, _):
         s = lax.rem(me + N - d, N)
@@ -223,26 +278,54 @@
 
     def far_copy(dst, idx):
         return pltpu.make_async_remote_copy(
-            src_ref=far_send.at[dst], dst_ref=far_out.at[pl.ds(SLOTS * idx, SLOTS)], send_sem=z_ss.at[dst],
+            src_ref=far_send.at[dst], dst_ref=far_out.at[pl.ds((SLOTS - RAW) * idx, SLOTS - RAW)], send_sem=z_ss.at[dst],
             recv_sem=z_rs.at[idx], device_id={"pb": dst}, device_id_type=MESH)
 
     def select(d, _):
-        half = lax.div(d + 1, 2)
-        off = 8 + half * (2 * lax.rem(d, 2) - 1)
-        dst = lax.rem(grp + off, N)
-        for k in range(SLOTS):
-            far_send[dst, k] = kv_out[jnp.clip(tab[GROUP + dst, k], 0, GROUP - 1)]
+        dst = lax.rem(grp + off_of(d), N)
+        for k in range(RAW, SLOTS):
+            far_send[dst, k - RAW] = kv_out[wanted(dst, k)]
         far_copy(dst, grp).start()
         return 0
 
     lax.fori_loop(0, N - 1, select, 0)
-    far_out[pl.ds(SLOTS * grp, SLOTS)] = kv_out[0:SLOTS]
+    far_out[pl.ds((SLOTS - RAW) * grp, SLOTS - RAW)] = kv_out[0:SLOTS - RAW]
+
+    def part_arrive(d, _):
+        s = lax.rem(grp + N - d, N)
+        far_part(s, s).wait_recv()
+        return 0
+
+    lax.fori_loop(1, N, part_arrive, 0)
+
+    def raw_copy(dst, idx):
+        return pltpu.make_async_remote_copy(
+            src_ref=raw_send.at[dst], dst_ref=raw_got.at[idx], send_sem=r_ss.at[dst],
+            recv_sem=r_rs.at[idx], device_id={"sp": dst}, device_id_type=MESH)
+
+    def project_raw(i, _):
+        p = pair(i)
+        x = part_far[...].reshape(N * RAW * PART, D)
+        y = jnp.dot(x, w_buf[p], preferred_element_type=jnp.float32)
+        for k in range(2):
+            h = 2 * p + k
+            o = k * 192
+            raw_send[h] = y[:, o + 64:o + 192].astype(jnp.bfloat16)
+
+            @pl.when(h != me)
+            def _():
+                raw_copy(h, me).start()
+        return 0
+
+    lax.fori_loop(0, 8, project_raw, 0)
+    raw_got[me] = raw_send[me]
 
     def drain(d, _):
         s = lax.rem(me + N - d, N)
         q_copy(s, s).wait_recv()
         q_copy(s, s).wait_send()
         kv_copy(me, s, s).wait_send()
+        part_copy(s, s).wait_send()
         return 0
 
     lax.fori_loop(1, N, drain, 0)
@@ -256,30 +339,53 @@
 
     lax.fori_loop(0, N, setup, 0)
 
-    def fetch(r, c):
-        row = jnp.minimum(r, GROUP - 1)
-        return jnp.concatenate(
-            [kv_out[jnp.clip(tab[row, c + t], 0, GROUP - 1)] for t in range(CHUNK)], axis=0)
+    def fetch_from(base):
+        def fetch(r, c):
+            row = jnp.minimum(r, HALF - 1) + base
+            return jnp.concatenate(
+                [kv_out[jnp.clip(tab[row, c + t], 0, GROUP - 1)] for t in range(CHUNK)], axis=0)
+        return fetch
 
     per_row = EARLY // CHUNK
-    steps = GROUP * per_row
+    steps = HALF * per_row
 
     def item(i):
         valid = (i >= 0) & (i < steps)
         i = jnp.clip(i, 0, steps - 1)
         row = lax.div(i, per_row)
-        return jnp.where(valid, row, GROUP), (i - row * per_row) * CHUNK
+        return jnp.where(valid, row, HALF), (i - row * per_row) * CHUNK
 
     def advance(i, _):
-        run_stages(
-            lax.rem(i, 2), [item(i - k) for k in range(4)], fetch,
-            lambda row: tab[row, LISTED], qz, (acc, total, top), buffers)
+        items = [item(i - k) for k in range(4)]
+        for k in range(2):
+            run_stages(
+                lax.rem(i, 2), items, fetch_from(k * HALF), lambda row: tab[row, LISTED], qz,
+                k * HALF, states[k], buffers[6 * k:6 * k + 6])
         return 0
 
     lax.fori_loop(0, steps + 3, advance, 0)
+
+    def drain_raw(d, _):
+        s = lax.rem(me + N - d, N)
+        raw_copy(s, s).wait_recv()
+        raw_copy(s, s).wait_send()
+        return 0
+
+    lax.fori_loop(1, N, drain_raw, 0)
+
+    def assemble(o, _):
+        rows = pl.ds(pl.multiple_of(o * RAW * PART, RAW * PART), RAW * PART)
+        pieces = [raw_got[s, rows, :].astype(jnp.float32) for s in range(N)]
+        for k in range(RAW):
+            tile = jnp.concatenate([x[k * PART:(k + 1) * PART] for x in pieces], axis=0)
+            raw_out[o * RAW + k] = tile.astype(jnp.bfloat16)
+        return 0
+
+    lax.fori_loop(0, N, assemble, 0)
 
     def drain_far(d, _):
         s = lax.rem(grp + N - d, N)
+        far_part(s, s).wait_send()
         far_copy(s, s).wait_recv()
         far_copy(s, s).wait_send()
         return 0
@@ -287,112 +393,136 @@
     lax.fori_loop(1, N, drain_far, 0)
 
 
-def exchange(listed, count, nodes, project_in):
+def exchange(listed, count, nodes, parts, project_in):
     b16, f32, i32 = jnp.bfloat16, jnp.float32, jnp.int32
     vm = pl.BlockSpec(memory_space=pltpu.VMEM)
     dma = pltpu.SemaphoreType.DMA
-    state = jax.ShapeDtypeStruct((GROUP + 1, TILE, TILE), f32)
+    state = jax.ShapeDtypeStruct((HALF + 1, TILE, TILE), f32)
     return pl.pallas_call(
         exchange_kernel,
         out_shape=(
             jax.ShapeDtypeStruct((GROUP, TILE, TILE), b16),
             jax.ShapeDtypeStruct((GROUP, TILE, TILE), b16),
-            jax.ShapeDtypeStruct((N * SLOTS, TILE, TILE), b16),
+            jax.ShapeDtypeStruct((N * RAW, TILE, TILE), b16),
+            jax.ShapeDtypeStruct((N * (SLOTS - RAW), TILE, TILE), b16),
             jax.ShapeDtypeStruct((GROUP + N, TILE), i32),
-            state, state, state,
+            *[state] * 6,
         ),
-        in_specs=[pl.BlockSpec(memory_space=pltpu.HBM)] * 4,
-        out_specs=(vm,) * 7,
+        in_specs=[pl.BlockSpec(memory_space=pltpu.HBM)] * 5,
+        out_specs=(vm,) * 11,
         scratch_shapes=[
             pltpu.VMEM((8, D, 384), b16),
             pltpu.VMEM((N, 2, TILE, TILE), b16),
             pltpu.VMEM((N, TILE, TILE), b16),
             pltpu.VMEM((N, TILE, TILE), b16),
-            pltpu.VMEM((N, SLOTS, TILE, TILE), b16),
+            pltpu.VMEM((N, SLOTS - RAW, TILE, TILE), b16),
+            pltpu.VMEM((2, N, PART, D), b16),
+            pltpu.VMEM((GROUP, PART, D), b16),
+            pltpu.VMEM((N, RAW * PART, D), b16),
+            pltpu.VMEM((N, RAW * PART, D), b16),
+            pltpu.VMEM((N, N * RAW * PART, TILE), b16),
+            pltpu.VMEM((N, N * RAW * PART, TILE), b16),
             pltpu.VMEM((LISTED, N * GROUP), i32),
             pltpu.VMEM((1, N * GROUP), i32),
             pltpu.VMEM((2 * TILE, D), b16),
             pltpu.VMEM((N * GROUP, LISTED), i32),
             pltpu.SMEM((GROUP + N, TILE), i32),
-            dma((3,)), dma((8,)), dma((N,)), dma((N,)), dma((N,)), dma((N,)), dma((N,)), dma((N,)), dma,
+            dma((4,)), dma((8,)), *[dma((N,))] * 12, dma,
             *scratch_state(),
         ],
         compiler_params=pltpu.CompilerParams(
             collective_id=0, has_side_effects=True, vmem_limit_bytes=30 << 20),
         name="exchange",
-    )(listed, count, nodes, project_in)
-
-
-def attend_kernel(
-    tab, qz, kv_ref, far_ref, acc_in, total_in, top_in, out_ref, acc, total, top, kv, rows, *buffers,
-):
+    )(listed, count, nodes, parts, project_in)
+
+
+def attend_kernel(tab, qz, kv_ref, raw_ref, far_ref, *refs):
+    out_ref, acc_a, total_a, top_a, acc_b, total_b, top_b, kv, rows = refs[6:15]
+    buffers = refs[15:]
+    states = ((acc_a, total_a, top_a), (acc_b, total_b, top_b))
     kv[0:GROUP] = kv_ref[...]
-    kv[GROUP:] = far_ref[...]
+    kv[GROUP:GROUP + N * RAW] = raw_ref[...]
+    kv[GROUP + N * RAW:] = far_ref[...]
     lane = lax.broadcasted_iota(jnp.int32, (TILE, TILE), 1)
-    clear_stages(*buffers)
+    clear_stages(buffers)
 
     def first(r):
         return jnp.minimum(tab[r, LISTED], EARLY)
 
-    def gather(r, carry):
-        n, items = carry
-        left = tab[r, LISTED + 1] - first(r)
-        rows[n] = r
-        return n + jnp.where(left > 0, 1, 0), items + lax.div(left + CHUNK - 1, CHUNK)
-
-    used, items = lax.fori_loop(0, GROUP, gather, (jnp.int32(0), jnp.int32(0)))
-    rows[used] = GROUP
-
-    def fetch(r, c):
-        row = jnp.minimum(r, GROUP - 1)
-        return jnp.concatenate(
-            [kv[tab[row, jnp.minimum(c + t, LISTED - 1)]] for t in range(CHUNK)], axis=0)
+    used, items = [], []
+    for k in range(2):
+        def gather(r, carry, base=k * HALF, k=k):
+            n, total = carry
+            left = tab[r + base, LISTED + 1] - first(r + base)
+            rows[k, n] = r
+            return n + jnp.where(left > 0, 1, 0), total + lax.div(left + CHUNK - 1, CHUNK)
+
+        n, total = lax.fori_loop(0, HALF, gather, (jnp.int32(0), jnp.int32(0)), unroll=4)
+        rows[k, n] = HALF
+        used.append(n)
+        items.append(total)
+
+    def fetch_from(base):
+        def fetch(r, c):
+            row = jnp.minimum(r, HALF - 1) + base
+            return jnp.concatenate(
+                [kv[tab[row, jnp.minimum(c + t, LISTED - 1)]] for t in range(CHUNK)], axis=0)
+        return fetch
 
     def advance(i, state):
-        n, r0, c0, r1, c1, r2, c2, r3, c3 = state
-        run_stages(
-            lax.rem(i, 2), ((r0, c0), (r1, c1), (r2, c2), (r3, c3)), fetch,
-            lambda row: tab[row, LISTED + 1], qz, (acc, total, top), buffers)
-        row = jnp.minimum(r0, GROUP - 1)
-        more = (c0 + CHUNK < tab[row, LISTED + 1]) & (r0 < GROUP)
-        n = jnp.where(more, n, jnp.minimum(n + 1, used))
-        rn = jnp.where(more, r0, rows[n])
-        cn = jnp.where(more, c0 + CHUNK, first(jnp.minimum(rn, GROUP - 1)))
-        return n, rn, cn, r0, c0, r1, c1, r2, c2
-
-    r = rows[0]
-    zero, dummy = jnp.int32(0), jnp.int32(GROUP)
-    start = (zero, r, first(jnp.minimum(r, GROUP - 1)), dummy, zero, dummy, zero, dummy, zero)
-    lax.fori_loop(0, items + 3, advance, start)
+        following = []
+        for k in range(2):
+            n, r0, c0, r1, c1, r2, c2, r3, c3 = state[9 * k:9 * k + 9]
+            base = k * HALF
+            run_stages(
+                lax.rem(i, 2), ((r0, c0), (r1, c1), (r2, c2), (r3, c3)), fetch_from(base),
+                lambda row: tab[row, LISTED + 1], qz, base, states[k], buffers[6 * k:6 * k + 6])
+            row = jnp.minimum(r0, HALF - 1) + base
+            more = (c0 + CHUNK < tab[row, LISTED + 1]) & (r0 < HALF)
+            n = jnp.where(more, n, jnp.minimum(n + 1, used[k]))
+            rn = jnp.where(more, r0, rows[k, n])
+            cn = jnp.where(more, c0 + CHUNK, first(jnp.minimum(rn, HALF - 1) + base))
+            following += [n, rn, cn, r0, c0, r1, c1, r2, c2]
+        return tuple(following)
+
+    zero, dummy = jnp.int32(0), jnp.int32(HALF)
+    start = []
+    for k in range(2):
+        r = rows[k, 0]
+        start += [zero, r, first(jnp.minimum(r, HALF - 1) + k * HALF), dummy, zero, dummy, zero, dummy, zero]
+    lax.fori_loop(0, jnp.maximum(items[0], items[1]) + 3, advance, tuple(start))
+
+    def close(acc, total, r):
+        return acc[r] / jnp.sum(total[r], axis=1, keepdims=True)
 
     def finish(s, _):
-        even = acc[2 * s] / jnp.sum(total[2 * s], axis=1, keepdims=True)
-        odd = acc[2 * s + 1] / jnp.sum(total[2 * s + 1], axis=1, keepdims=True)
-        even = pltpu.roll(even, HEAD_DIM, 1)
-        out_ref[s] = jnp.where(lane < HEAD_DIM, even, odd).astype(jnp.bfloat16)
-        return 0
-
-    lax.fori_loop(0, N, finish, 0)
-
-
-def attend(tab, qz, kv, far, acc, total, top):
+        for k, (acc, total, _top) in enumerate(states):
+            even = pltpu.roll(close(acc, total, 2 * s), HEAD_DIM, 1)
+            odd = close(acc, total, 2 * s + 1)
+            out_ref[s + k * HALF // 2] = jnp.where(lane < HEAD_DIM, even, odd).astype(jnp.bfloat16)
+        return 0
+
+    lax.fori_loop(0, HALF // 2, finish, 0)
+
+
+def attend(tab, qz, kv, raw, far, *state):
     b16 = jnp.bfloat16
     vm = pl.BlockSpec(memory_space=pltpu.VMEM)
-    state = jax.ShapeDtypeStruct(acc.shape, acc.dtype)
+    kept = [jax.ShapeDtypeStruct(x.shape, x.dtype) for x in state]
     return pl.pallas_call(
         attend_kernel,
-        out_shape=(jax.ShapeDtypeStruct((N, TILE, TILE), b16), state, state, state),
-        in_specs=[pl.BlockSpec(memory_space=pltpu.SMEM)] + [vm] * 6,
-        out_specs=(vm,) * 4,
-        input_output_aliases={4: 1, 5: 2, 6: 3},
+        out_shape=(jax.ShapeDtypeStruct((N, TILE, TILE), b16), *kept),
+        in_specs=[pl.BlockSpec(memory_space=pltpu.SMEM)] + [vm] * 10,
+        out_specs=(vm,) * 7,
+        input_output_aliases={5 + i: 1 + i for i in range(6)},
         scratch_shapes=[
             pltpu.VMEM((GROUP + N * SLOTS, TILE, TILE), b16),
-            pltpu.SMEM((GROUP + 1,), jnp.int32),
+            pltpu.SMEM((2, HALF + 1), jnp.int32),
             *scratch_state(),
         ],
         compiler_params=pltpu.CompilerParams(vmem_limit_bytes=24 << 20),
         name="attend",
-    )(tab, qz, kv, far, acc, total, top)[0]
+    )(tab, qz, kv, raw, far, *state)[0]
 
 
 def finish_kernel(att_ref, nodes_ref, w_ref, out_ref, got, joined, ss, rs):
@@ -457,10 +587,11 @@
 
 
 def shards(nodes, project_in, project_out, tile_list, tile_count):
-    arguments = (tile_list.T, tile_count[None, :], nodes, project_in)
+    arguments = (
+        tile_list.T, tile_count[None, :], nodes, nodes.reshape(2, N, PART, D), project_in)
     arguments = [pltpu.with_memory_space_constraint(a, pltpu.HBM) for a in arguments]
-    qz, kv, far, tab, acc, total, top = exchange(*arguments)
-    att = attend(tab, qz, kv, far, acc, total, top)
+    qz, kv, raw, far, tab, *state = exchange(*arguments)
+    att = attend(tab, qz, kv, raw, far, *state)
     return finish(att, nodes, project_out)
 
 

time: 103 us -> 84.7 us (0.82)
  Pallas kernels: 103 us -> 83.4 us
    pallas_call x1, Pallas kernels: 72.8 us -> 60.4 us  [exchange(): pl.pallas_call(exchange_kernel, out_shape=(jax.ShapeDtypeStruct((GROUP, T...]
    pallas_call x1, Pallas kernels: 17.1 us -> 12.7 us  [attend(): pl.pallas_call(attend_kernel, out_shape=(jax.ShapeDtypeStruct((N, TILE, T...]
    pallas_call x1, Pallas kernels: 12.7 us -> 10.3 us  [finish(): pl.pallas_call(finish_kernel, out_shape=jax.ShapeDtypeStruct((2 * TILE, D...]
where the time goes in v1:
time: 84.7 us; the launch traced here: 84.2 us
  Pallas kernels  83.4 us (98%)
    pallas_call x1, Pallas kernels, exchange(): pl.pallas_call(exchange_kernel, out_shape=(jax.ShapeDtypeStruct((GROUP, T...  60.4 us
    pallas_call x1, Pallas kernels, attend(): pl.pallas_call(attend_kernel, out_shape=(jax.ShapeDtypeStruct((N, TILE, T...  12.7 us
    pallas_call x1, Pallas kernels, finish(): pl.pallas_call(finish_kernel, out_shape=jax.ShapeDtypeStruct((2 * TILE, D...  10.3 us

profile of v1, /device:TPU:8, one launch (start us, length us, event | category | flops | bytes accessed | tf_op | source)
XLA Modules:
  0.0 84.2 jit_solution(8842588209536245598)
XLA Ops:
  0.0 60.4 %exchange.1 = (bf16[32,128,128]{2,1,0:T(8,128)(2,1)S(1)}, bf16[32,128,128]{2,1,0:T(8,128)(2,1)S(1)}, bf16[32,128,128]{2,1,0:T(8,128)(2,1)S(1)}, bf16[32,128,128]...) custom-call(s32[32,512]{1,0:T(8,128)} %bitcast.4, ...), custom_call_target="tpu_custom_call" | custom-call | tf_op jit(solution)/shard_map/exchange/pallas_call | solution.py:401
  60.4 0.0 copy-start
  60.4 0.0 copy-start.1
  60.4 12.7 %attend.1 = (bf16[16,128,128]{2,1,0:T(8,128)(2,1)S(1)}, f32[17,128,128]{2,1,0:T(8,128)S(1)}, f32[17,128,128]{2,1,0:T(8,128)S(1)}, f32[17,128,128]{2,1,0:T(8,128)...) custom-call(s32[48,128]{1,0:T(8,128)S(1)} %get-tuple-element.17.tab,, ...), custom_call_target="tpu_custom_call", output_to_operand_aliasing={{1}: (5, {}), {2}: (6, {}), {3}: (7, {}), {4}: (8, {}), {5}... | custom-call | tf_op jit(solution)/shard_map/attend/pallas_call | solution.py:512
  73.1 0.0 copy-done
  73.1 0.0 copy-done.1
  73.1 10.3 %finish.1 = bf16[256,1024]{1,0:T(8,128)(2,1)S(1)} custom-call(bf16[16,128,128]{2,1,0:T(8,128)(2,1)S(1)} %get-tuple-element.28.att_ref, bf16[256,1024]{1,0:T(8,128)(2,1)S(1)} %copy-done, bf16[1024,1024]{1,0:T(8,128)(2,1)S(1)} %copy-done.1), custom_call_target="tpu_custom_call" | custom-call | tf_op jit(solution)/shard_map/finish/pallas_call | solution.py:573
  83.4 0.8 copy.19
Async XLA Ops:
  60.4 12.7 %copy-start = (bf16[256,1024]{1,0:T(8,128)(2,1)S(1)}, bf16[256,1024]{1,0:T(8,128)(2,1)}, u32[]{:S(2)}) copy-start(bf16[256,1024]{1,0:T(8,128)(2,1)} %nodes_ref.1) | copy-start | bytes 1572868
  60.4 12.7 %copy-start.1 = (bf16[1024,1024]{1,0:T(8,128)(2,1)S(1)}, bf16[1024,1024]{1,0:T(8,128)(2,1)}, u32[]{:S(2)}) copy-start(bf16[1024,1024]{1,0:T(8,128)(2,1)} %w_ref.1) | copy-start | bytes 6291460

commit v2 on v1

--- a/solution.py
+++ b/solution.py
@@ -24,28 +24,39 @@
 MESH = pl.DeviceIdType.MESH
 
 
-def build_tables(list_ref, count_ref, marked_ref, tab_ref, grp):
+def list_sends(list_ref, count_ref, live_ref, used_ref, send_ref, grp):
+    f32, b16, i32 = jnp.float32, jnp.bfloat16, jnp.int32
+    tiles = N * GROUP
+    places = lax.broadcasted_iota(i32, (LISTED, tiles), 0)
+    live_ref[...] = jnp.where(places < count_ref[...], list_ref[...], -1)
+
+    def uses(i, _):
+        hit = jnp.where(live_ref[...] == grp * GROUP + i, 1.0, 0.0)
+        used_ref[pl.ds(i, 1), :] = jnp.max(hit, axis=0, keepdims=True)
+        return 0
+
+    lax.fori_loop(0, GROUP, uses, 0, unroll=8)
+    row = lax.broadcasted_iota(i32, (tiles, TILE), 0)
+    lane = lax.broadcasted_iota(i32, (tiles, TILE), 1)
+    groups = jnp.where(lax.div(row, GROUP) == lane, 1.0, 0.0).astype(b16)
+    used = jnp.dot(used_ref[...].astype(b16), groups, preferred_element_type=f32)
+    used = jnp.where(used > 0, 1.0, 0.0)
+    up = lax.broadcasted_iota(i32, (GROUP, GROUP), 0)
+    across = lax.broadcasted_iota(i32, (GROUP, GROUP), 1)
+    before = jnp.where(across < up, 1.0, 0.0).astype(b16)
+    rank = jnp.dot(before, used.astype(b16), preferred_element_type=f32)
+    index = lax.broadcasted_iota(i32, (GROUP, TILE), 0).astype(f32)
+    for k in range(SLOTS):
+        pick = jnp.where((rank == k) & (used > 0), index, 0.0)
+        send_ref[k:k + 1, :] = jnp.sum(pick, axis=0, keepdims=True).astype(i32)
+
+
+def build_tables(live_ref, marked_ref, tab_ref, grp):
     f32, b16, i32 = jnp.float32, jnp.bfloat16, jnp.int32
     base = grp * GROUP
-    places = lax.broadcasted_iota(i32, (LISTED, N * GROUP), 0)
-    across = jnp.where(places < count_ref[...], list_ref[...], -1)
+    across = live_ref[...]
     for b in range(0, N * GROUP, TILE):
         marked_ref[b:b + TILE, :] = across[:, b:b + TILE].T
-    lane = lax.broadcasted_iota(i32, (N, TILE), 1)
-
-    def uses(i, used):
-        hit = jnp.where(marked_ref[...] == base + i, 1.0, 0.0)
-        hit = jnp.max(hit.reshape(N, GROUP, LISTED), axis=1)
-        return jnp.where(lane == i, jnp.max(hit, axis=1, keepdims=True), used)
-
-    used = lax.fori_loop(0, GROUP, uses, jnp.zeros((N, TILE), f32), unroll=4)
-    low = lax.broadcasted_iota(i32, (TILE, TILE), 0) < lax.broadcasted_iota(i32, (TILE, TILE), 1)
-    rank = jnp.dot(used.astype(b16), jnp.where(low, 1.0, 0.0).astype(b16), preferred_element_type=f32)
-    send = jnp.zeros((N, TILE), f32)
-    for k in range(SLOTS):
-        pick = jnp.where((rank == k) & (used > 0), lane.astype(f32), 0.0)
-        send = jnp.where(lane == k, jnp.sum(pick, axis=1, keepdims=True), send)
-    tab_ref[GROUP:] = send.astype(i32)
     tiles = N * GROUP
     own = marked_ref[pl.ds(pl.multiple_of(base, GROUP), GROUP), :]
     tile = lax.broadcasted_iota(i32, (GROUP, tiles), 1)
@@ -82,14 +93,14 @@
     out = lax.fori_loop(0, LISTED, place, jnp.zeros((GROUP, TILE), f32), unroll=4)
     out = jnp.where(wide == LISTED, near_count, out)
     out = jnp.where(wide == LISTED + 1, count, out)
-    tab_ref[:GROUP] = out.astype(i32)
+    tab_ref[...] = out.astype(i32)
 
 
 def scratch_state():
     f32 = jnp.float32
     square = pltpu.VMEM((TILE, TILE), f32)
-    return 2 * [
-        pltpu.VMEM((2, TILE, CHUNK * TILE), f32),
+    return 4 * [
+        pltpu.VMEM((TILE, CHUNK * TILE), f32),
         pltpu.VMEM((TILE, CHUNK * TILE), jnp.bfloat16),
         square, square, square, square,
     ]
@@ -100,24 +111,29 @@
         ref[...] = jnp.zeros_like(ref)
 
 
-def run_stages(slot, items, fetch, live, qz, base, state, buffers):
+def stream_buffers(buffers, k):
+    return buffers[12 * k:12 * k + 6], buffers[12 * k + 6:12 * k + 12]
+
+
+def run_stages(items, fetch, live, qz, base, state, here, there):
     acc, total, top = state
-    s_buf, p_buf, m_cur, m_max, a_cur, a_old = buffers
+    s_buf, p_buf, m_cur, m_max, a_cur, a_old = here
+    _, p_last, m_last, m_max_last, a_last, a_old_last = there
     (r0, c0), (r1, _), (r2, _), (r3, c3) = items
-    added = jnp.dot(p_buf[...], fetch(r3, c3), preferred_element_type=jnp.float32)
-    acc[r3] = acc[r3] * a_old[...] + added
-    m = m_cur[...]
-    fade = a_cur[...]
+    added = jnp.dot(p_last[...], fetch(r3, c3), preferred_element_type=jnp.float32)
+    acc[r3] = acc[r3] * a_old_last[...] + added
+    m = m_last[...]
+    fade = a_last[...]
     part = None
     for t in range(CHUNK):
         cols = slice(t * TILE, (t + 1) * TILE)
-        w = jnp.exp(s_buf[slot, :, cols] - m)
+        w = jnp.exp(s_buf[:, cols] - m)
         p_buf[:, cols] = w.astype(jnp.bfloat16)
         part = w if part is None else part + w
     total[r2] = total[r2] * fade + part
     a_old[...] = fade
     before = top[r1]
-    now = jnp.maximum(before, jnp.max(m_max[...], axis=1, keepdims=True))
+    now = jnp.maximum(before, jnp.max(m_max_last[...], axis=1, keepdims=True))
     top[r1] = now
     m_cur[...] = now
     a_cur[...] = jnp.exp(before - now)
@@ -128,17 +144,21 @@
     for t in range(CHUNK):
         cols = slice(t * TILE, (t + 1) * TILE)
         st = s[:, cols] + jnp.where(c0 + t < live(row), 0.0, LOW)
-        s_buf[slot, :, cols] = st
+        s_buf[:, cols] = st
         big = st if big is None else jnp.maximum(big, st)
     m_max[...] = big
+
+
+def shifted(me, d):
+    return lax.rem(me // 4 + d // 4, 4) * 4 + lax.rem(lax.rem(me, 4) + lax.rem(d, 4), 4)
 
 
 def exchange_kernel(
     list_hbm, count_hbm, nodes_hbm, parts_hbm, w_hbm,
     qz, kv_out, raw_out, far_out, tab_out, acc_a, total_a, top_a, acc_b, total_b, top_b,
     w_buf, kv_send, q_send, q_got, far_send, parts, part_got, part_send, part_far, raw_send, raw_got,
-    list_ref, count_ref, nodes_ref, marked, tab, in_sem, w_sem, kv_ss, kv_rs, q_ss, q_rs, z_ss, z_rs,
-    p_ss, p_rs, y_ss, y_rs, r_ss, r_rs, t_sem,
+    list_ref, count_ref, nodes_ref, live_ref, used_ref, sends_ref, marked, sends, tab, in_sem, w_sem, kv_ss, kv_rs, q_ss, q_rs, z_ss, z_rs,
+    p_ss, p_rs, y_ss, y_rs, r_ss, r_rs, t_sem, u_sem,
     *buffers,
 ):
     me = lax.axis_index("sp")
@@ -149,7 +169,7 @@
         return pltpu.make_async_copy(w_hbm.at[:, cols], w_buf.at[p], w_sem.at[p])
 
     def pair(i):
-        return lax.rem(me // 2 + i, 8)
+        return lax.rem(me // 4 + i // 2, 4) * 2 + lax.rem(lax.rem(me, 4) // 2 + i, 2)
 
     arrivals = [
         pltpu.make_async_copy(a, b, in_sem.at[i])
@@ -169,6 +189,11 @@
         return 0
 
     lax.fori_loop(1, N, greet, 0)
+    arrivals[2].wait()
+    arrivals[3].wait()
+    list_sends(list_ref, count_ref, live_ref, used_ref, sends_ref, grp)
+    sends_copy = pltpu.make_async_copy(sends_ref, sends, u_sem)
+    sends_copy.start()
     pl.semaphore_wait(barrier, 2 * (N - 1))
 
     def kv_copy(src, dst, idx):
@@ -203,27 +228,56 @@
             recv_sem=p_rs.at[idx], device_id={"sp": dst}, device_id_type=MESH)
 
     def send_part(d, _):
-        part_copy(lax.rem(me + d, N), me).start()
+        part_copy(shifted(me, d), me).start()
         return 0
 
     arrivals[0].wait()
     lax.fori_loop(1, N, send_part, 0)
     own_part = pltpu.make_async_copy(parts.at[:, me], part_got.at[pl.ds(2 * me, 2)], in_sem.at[0])
     own_part.start()
-    for copy in arrivals[1:]:
-        copy.wait()
+    arrivals[1].wait()
     lax.fori_loop(0, 8, project, 0)
     own_part.wait()
     kv_out[pl.ds(2 * me, 2)] = kv_send[me]
     q_got[me] = q_send[me]
 
     def send_q(d, _):
-        q_copy(lax.rem(me + d, N), me).start()
+        q_copy(shifted(me, d), me).start()
         return 0
 
     lax.fori_loop(1, N, send_q, 0)
 
-    build_tables(list_ref, count_ref, marked, tab_out, grp)
+    sends_copy.wait()
+
+    def off_of(d):
+        half = lax.div(d + 1, 2)
+        return 8 + half * (2 * lax.rem(d, 2) - 1)
+
+    def part_wait(d, _):
+        s = lax.rem(me + N - d, N)
+        part_copy(s, s).wait_recv()
+        return 0
+
+    lax.fori_loop(1, N, part_wait, 0)
+
+    def wanted(dst, k):
+        return jnp.clip(sends[k, dst], 0, GROUP - 1)
+
+    def far_part(dst, idx):
+        return pltpu.make_async_remote_copy(
+            src_ref=part_send.at[dst], dst_ref=part_far.at[idx], send_sem=y_ss.at[dst],
+            recv_sem=y_rs.at[idx], device_id={"pb": dst}, device_id_type=MESH)
+
+    def select_part(d, _):
+        dst = lax.rem(grp + off_of(d), N)
+        rows = [part_got[wanted(dst, k)].astype(jnp.float32) for k in range(RAW)]
+        part_send[dst] = jnp.concatenate(rows, axis=0).astype(jnp.bfloat16)
+        far_part(dst, grp).start()
+        return 0
+
+    lax.fori_loop(0, N - 1, select_part, 0)
+    part_far[grp] = jnp.zeros((RAW * PART, D), jnp.bfloat16)
+    build_tables(live_ref, marked, tab_out, grp)
     to_scalar = pltpu.make_async_copy(tab_out, tab, t_sem)
     to_scalar.start()
 
@@ -240,34 +294,6 @@
     clear_stages(buffers)
     to_scalar.wait()
 
-    def off_of(d):
-        half = lax.div(d + 1, 2)
-        return 8 + half * (2 * lax.rem(d, 2) - 1)
-
-    def part_wait(d, _):
-        s = lax.rem(me + N - d, N)
-        part_copy(s, s).wait_recv()
-        return 0
-
-    lax.fori_loop(1, N, part_wait, 0)
-
-    def wanted(dst, k):
-        return jnp.clip(tab[GROUP + dst, k], 0, GROUP - 1)
-
-    def far_part(dst, idx):
-        return pltpu.make_async_remote_copy(
-            src_ref=part_send.at[dst], dst_ref=part_far.at[idx], send_sem=y_ss.at[dst],
-            recv_sem=y_rs.at[idx], device_id={"pb": dst}, device_id_type=MESH)
-
-    def select_part(d, _):
-        dst = lax.rem(grp + off_of(d), N)
-        rows = [part_got[wanted(dst, k)].astype(jnp.float32) for k in range(RAW)]
-        part_send[dst] = jnp.concatenate(rows, axis=0).astype(jnp.bfloat16)
-        far_part(dst, grp).start()
-        return 0
-
-    lax.fori_loop(0, N - 1, select_part, 0)
-    part_far[grp] = jnp.zeros((RAW * PART, D), jnp.bfloat16)
 
     def wait_kv(d, _):
         s = lax.rem(me + N - d, N)
@@ -323,12 +349,10 @@
     def drain(d, _):
         s = lax.rem(me + N - d, N)
         q_copy(s, s).wait_recv()
-        q_copy(s, s).wait_send()
-        kv_copy(me, s, s).wait_send()
-        part_copy(s, s).wait_send()
         return 0
 
     lax.fori_loop(1, N, drain, 0)
+
     zero64 = jnp.zeros((TILE, HEAD_DIM), jnp.bfloat16)
 
     def setup(s, _):
@@ -355,20 +379,25 @@
         row = lax.div(i, per_row)
         return jnp.where(valid, row, HALF), (i - row * per_row) * CHUNK
 
-    def advance(i, _):
-        items = [item(i - k) for k in range(4)]
-        for k in range(2):
-            run_stages(
-                lax.rem(i, 2), items, fetch_from(k * HALF), lambda row: tab[row, LISTED], qz,
-                k * HALF, states[k], buffers[6 * k:6 * k + 6])
-        return 0
-
-    lax.fori_loop(0, steps + 3, advance, 0)
+    def advance(j, _):
+        for odd in range(2):
+            items = [item(2 * j + odd - k) for k in range(4)]
+            for k in range(2):
+                pair_of = stream_buffers(buffers, k)
+                run_stages(
+                    items, fetch_from(k * HALF), lambda row: tab[row, LISTED], qz,
+                    k * HALF, states[k], pair_of[odd], pair_of[1 - odd])
+        return 0
+
+    lax.fori_loop(0, (steps + 4) // 2, advance, 0)
 
     def drain_raw(d, _):
         s = lax.rem(me + N - d, N)
         raw_copy(s, s).wait_recv()
         raw_copy(s, s).wait_send()
+        q_copy(s, s).wait_send()
+        kv_copy(me, s, s).wait_send()
+        part_copy(s, s).wait_send()
         return 0
 
     lax.fori_loop(1, N, drain_raw, 0)
@@ -405,7 +434,7 @@
             jax.ShapeDtypeStruct((GROUP, TILE, TILE), b16),
             jax.ShapeDtypeStruct((N * RAW, TILE, TILE), b16),
             jax.ShapeDtypeStruct((N * (SLOTS - RAW), TILE, TILE), b16),
-            jax.ShapeDtypeStruct((GROUP + N, TILE), i32),
+            jax.ShapeDtypeStruct((GROUP, TILE), i32),
             *[state] * 6,
         ),
         in_specs=[pl.BlockSpec(memory_space=pltpu.HBM)] * 5,
@@ -425,9 +454,13 @@
             pltpu.VMEM((LISTED, N * GROUP), i32),
             pltpu.VMEM((1, N * GROUP), i32),
             pltpu.VMEM((2 * TILE, D), b16),
+            pltpu.VMEM((LISTED, N * GROUP), i32),
+            pltpu.VMEM((GROUP, N * GROUP), f32),
+            pltpu.VMEM((SLOTS, TILE), i32),
             pltpu.VMEM((N * GROUP, LISTED), i32),
-            pltpu.SMEM((GROUP + N, TILE), i32),
-            dma((4,)), dma((8,)), *[dma((N,))] * 12, dma,
+            pltpu.SMEM((SLOTS, TILE), i32),
+            pltpu.SMEM((GROUP, TILE), i32),
+            dma((4,)), dma((8,)), *[dma((N,))] * 12, dma, dma,
             *scratch_state(),
         ],
         compiler_params=pltpu.CompilerParams(
@@ -469,28 +502,30 @@
                 [kv[tab[row, jnp.minimum(c + t, LISTED - 1)]] for t in range(CHUNK)], axis=0)
         return fetch
 
-    def advance(i, state):
-        following = []
-        for k in range(2):
-            n, r0, c0, r1, c1, r2, c2, r3, c3 = state[9 * k:9 * k + 9]
-            base = k * HALF
-            run_stages(
-                lax.rem(i, 2), ((r0, c0), (r1, c1), (r2, c2), (r3, c3)), fetch_from(base),
-                lambda row: tab[row, LISTED + 1], qz, base, states[k], buffers[6 * k:6 * k + 6])
-            row = jnp.minimum(r0, HALF - 1) + base
-            more = (c0 + CHUNK < tab[row, LISTED + 1]) & (r0 < HALF)
-            n = jnp.where(more, n, jnp.minimum(n + 1, used[k]))
-            rn = jnp.where(more, r0, rows[k, n])
-            cn = jnp.where(more, c0 + CHUNK, first(jnp.minimum(rn, HALF - 1) + base))
-            following += [n, rn, cn, r0, c0, r1, c1, r2, c2]
-        return tuple(following)
+    def advance(_, state):
+        state = list(state)
+        for odd in range(2):
+            for k in range(2):
+                n, r0, c0, r1, c1, r2, c2, r3, c3 = state[9 * k:9 * k + 9]
+                base = k * HALF
+                pair_of = stream_buffers(buffers, k)
+                run_stages(
+                    ((r0, c0), (r1, c1), (r2, c2), (r3, c3)), fetch_from(base),
+                    lambda row: tab[row, LISTED + 1], qz, base, states[k], pair_of[odd], pair_of[1 - odd])
+                row = jnp.minimum(r0, HALF - 1) + base
+                more = (c0 + CHUNK < tab[row, LISTED + 1]) & (r0 < HALF)
+                n = jnp.where(more, n, jnp.minimum(n + 1, used[k]))
+                rn = jnp.where(more, r0, rows[k, n])
+                cn = jnp.where(more, c0 + CHUNK, first(jnp.minimum(rn, HALF - 1) + base))
+                state[9 * k:9 * k + 9] = [n, rn, cn, r0, c0, r1, c1, r2, c2]
+        return tuple(state)
 
     zero, dummy = jnp.int32(0), jnp.int32(HALF)
     start = []
     for k in range(2):
         r = rows[k, 0]
         start += [zero, r, first(jnp.minimum(r, HALF - 1) + k * HALF), dummy, zero, dummy, zero, dummy, zero]
-    lax.fori_loop(0, jnp.maximum(items[0], items[1]) + 3, advance, tuple(start))
+    lax.fori_loop(0, lax.div(jnp.maximum(items[0], items[1]) + 4, 2), advance, tuple(start))
 
     def close(acc, total, r):
         return acc[r] / jnp.sum(total[r], axis=1, keepdims=True)

time: 84.7 us -> 81 us (0.956)
  the two profiles are of different devices: /device:TPU:8 before, /device:TPU:1 now
where the time goes in v2:
time: 81 us; the launch traced here: 81.5 us
  Pallas kernels  80.6 us (100%)
  local copies, waits for them, and re-layouts  0.81 us (1%)
    pallas_call x1, Pallas kernels, exchange(): pl.pallas_call(exchange_kernel, out_shape=(jax.ShapeDtypeStruct((GROUP, T...  56.8 us
    pallas_call x1, Pallas kernels, attend(): pl.pallas_call(attend_kernel, out_shape=(jax.ShapeDtypeStruct((N, TILE, T...  12 us
    pallas_call x1, Pallas kernels, finish(): pl.pallas_call(finish_kernel, out_shape=jax.ShapeDtypeStruct((2 * TILE, D...  11.9 us

profile of v2, /device:TPU:1, one launch (start us, length us, event | category | flops | bytes accessed | tf_op | source)
XLA Modules:
  0.0 81.5 jit_solution(2011269940216374053)
XLA Ops:
  0.0 56.8 %exchange.1 = (bf16[32,128,128]{2,1,0:T(8,128)(2,1)S(1)}, bf16[32,128,128]{2,1,0:T(8,128)(2,1)S(1)}, bf16[32,128,128]{2,1,0:T(8,128)(2,1)S(1)}, bf16[32,128,128]...) custom-call(s32[32,512]{1,0:T(8,128)} %bitcast.4, ...), custom_call_target="tpu_custom_call" | custom-call | tf_op jit(solution)/shard_map/exchange/pallas_call | solution.py:430
  56.8 0.0 copy-start
  56.8 0.0 copy-start.1
  56.8 12.0 %attend.1 = (bf16[16,128,128]{2,1,0:T(8,128)(2,1)S(1)}, f32[17,128,128]{2,1,0:T(8,128)S(1)}, f32[17,128,128]{2,1,0:T(8,128)S(1)}, f32[17,128,128]{2,1,0:T(8,128)...) custom-call(s32[32,128]{1,0:T(8,128)S(1)} %get-tuple-element.17.tab,, ...), custom_call_target="tpu_custom_call", output_to_operand_aliasing={{1}: (5, {}), {2}: (6, {}), {3}: (7, {}), {4}: (8, {}), {5}... | custom-call | tf_op jit(solution)/shard_map/attend/pallas_call | solution.py:547
  68.8 0.0 copy-done
  68.8 0.0 copy-done.1
  68.8 11.9 %finish.1 = bf16[256,1024]{1,0:T(8,128)(2,1)S(1)} custom-call(bf16[16,128,128]{2,1,0:T(8,128)(2,1)S(1)} %get-tuple-element.28.att_ref, bf16[256,1024]{1,0:T(8,128)(2,1)S(1)} %copy-done, bf16[1024,1024]{1,0:T(8,128)(2,1)S(1)} %copy-done.1), custom_call_target="tpu_custom_call" | custom-call | tf_op jit(solution)/shard_map/finish/pallas_call | solution.py:608
  80.7 0.8 copy.19
Async XLA Ops:
  56.8 12.0 %copy-start = (bf16[256,1024]{1,0:T(8,128)(2,1)S(1)}, bf16[256,1024]{1,0:T(8,128)(2,1)}, u32[]{:S(2)}) copy-start(bf16[256,1024]{1,0:T(8,128)(2,1)} %nodes_ref.1) | copy-start | bytes 1572868
  56.8 12.0 %copy-start.1 = (bf16[1024,1024]{1,0:T(8,128)(2,1)S(1)}, bf16[1024,1024]{1,0:T(8,128)(2,1)}, u32[]{:S(2)}) copy-start(bf16[1024,1024]{1,0:T(8,128)(2,1)} %w_ref.1) | copy-start | bytes 6291460

commit v3 on v2

--- a/solution.py
+++ b/solution.py
@@ -17,6 +17,8 @@
 N = 16
 CHUNK = 4
 EARLY = 8
+LATE = 32
+COUNTS = 64
 HALF = GROUP // 2
 RAW = 2
 PART = TILE // N
@@ -73,16 +75,18 @@
     rank = jnp.dot(wanted.astype(b16), same, preferred_element_type=f32)[0:1]
     owner = lax.div(tile, GROUP)
     here = owner == grp
-    raw = (GROUP + RAW * owner).astype(f32) + rank
-    cooked = (GROUP + RAW * N - RAW + (SLOTS - RAW) * owner).astype(f32) + rank
-    slot = jnp.where(here, (tile - base).astype(f32), jnp.where(rank < RAW, raw, cooked))
+    first = (GROUP + RAW * owner).astype(f32) + rank
+    second = (GROUP + RAW * N - RAW + (SLOTS - RAW) * owner).astype(f32) + rank
+    slot = jnp.where(here, (tile - base).astype(f32), jnp.where(rank < RAW, first, second))
     near = jnp.where(here, present, 0.0)
-    away = jnp.where(here, 0.0, present)
-    both = jnp.concatenate([near, away], axis=0).astype(b16)
+    raw = jnp.where(jnp.logical_not(here) & (rank < RAW), present, 0.0)
+    both = jnp.concatenate([near, raw], axis=0).astype(b16)
     order = jnp.dot(both, before, preferred_element_type=f32)
-    near_count = jnp.sum(near, axis=1, keepdims=True)
-    count = jnp.sum(present, axis=1, keepdims=True)
-    order = jnp.where(here, order[:GROUP], order[GROUP:] + near_count)
+    near = jnp.where(order[:GROUP] < EARLY, near, 0.0)
+    raw = jnp.where(order[GROUP:] < CHUNK, raw, 0.0)
+    late = present - near - raw
+    last = jnp.dot(late.astype(b16), before, preferred_element_type=f32) + LATE
+    order = jnp.where(near > 0, order[:GROUP], jnp.where(raw > 0, order[GROUP:] + EARLY, last))
     order = jnp.where(present > 0, order, -1.0)
     wide = lax.broadcasted_iota(i32, (GROUP, TILE), 1)
 
@@ -90,9 +94,10 @@
         v = jnp.sum(jnp.where(order == k.astype(f32), slot, 0.0), axis=1, keepdims=True)
         return jnp.where(wide == k, v, out)
 
-    out = lax.fori_loop(0, LISTED, place, jnp.zeros((GROUP, TILE), f32), unroll=4)
-    out = jnp.where(wide == LISTED, near_count, out)
-    out = jnp.where(wide == LISTED + 1, count, out)
+    out = lax.fori_loop(0, EARLY + CHUNK, place, jnp.zeros((GROUP, TILE), f32), unroll=4)
+    out = lax.fori_loop(LATE, LATE + LISTED, place, out, unroll=4)
+    for i, kind in enumerate((near, raw, late)):
+        out = jnp.where(wide == COUNTS + i, jnp.sum(kind, axis=1, keepdims=True), out)
     tab_ref[...] = out.astype(i32)
 
 
@@ -363,44 +368,43 @@
 
     lax.fori_loop(0, N, setup, 0)
 
-    def fetch_from(base):
-        def fetch(r, c):
-            row = jnp.minimum(r, HALF - 1) + base
-            return jnp.concatenate(
-                [kv_out[jnp.clip(tab[row, c + t], 0, GROUP - 1)] for t in range(CHUNK)], axis=0)
-        return fetch
-
-    per_row = EARLY // CHUNK
-    steps = HALF * per_row
-
-    def item(i):
-        valid = (i >= 0) & (i < steps)
-        i = jnp.clip(i, 0, steps - 1)
-        row = lax.div(i, per_row)
-        return jnp.where(valid, row, HALF), (i - row * per_row) * CHUNK
-
-    def advance(j, _):
-        for odd in range(2):
-            items = [item(2 * j + odd - k) for k in range(4)]
-            for k in range(2):
-                pair_of = stream_buffers(buffers, k)
-                run_stages(
-                    items, fetch_from(k * HALF), lambda row: tab[row, LISTED], qz,
-                    k * HALF, states[k], pair_of[odd], pair_of[1 - odd])
-        return 0
-
-    lax.fori_loop(0, (steps + 4) // 2, advance, 0)
-
-    def drain_raw(d, _):
+    def attend_early(per_row, at, table, offset, lane):
+        steps = HALF * per_row
+
+        def fetch_from(base):
+            def fetch(r, c):
+                row = jnp.minimum(r, HALF - 1) + base
+                last = table.shape[0] - 1
+                return jnp.concatenate(
+                    [table[jnp.clip(tab[row, c + t] - offset, 0, last)] for t in range(CHUNK)], axis=0)
+            return fetch
+
+        def item(i):
+            valid = (i >= 0) & (i < steps)
+            i = jnp.clip(i, 0, steps - 1)
+            row = lax.div(i, per_row)
+            return jnp.where(valid, row, HALF), at + (i - row * per_row) * CHUNK
+
+        def advance(j, _):
+            for odd in range(2):
+                items = [item(2 * j + odd - k) for k in range(4)]
+                for k in range(2):
+                    pair_of = stream_buffers(buffers, k)
+                    run_stages(
+                        items, fetch_from(k * HALF), lambda row: at + tab[row, lane], qz,
+                        k * HALF, states[k], pair_of[odd], pair_of[1 - odd])
+            return 0
+
+        lax.fori_loop(0, (steps + 4) // 2, advance, 0)
+
+    attend_early(EARLY // CHUNK, 0, kv_out, 0, COUNTS)
+
+    def arrive_raw(d, _):
         s = lax.rem(me + N - d, N)
         raw_copy(s, s).wait_recv()
-        raw_copy(s, s).wait_send()
-        q_copy(s, s).wait_send()
-        kv_copy(me, s, s).wait_send()
-        part_copy(s, s).wait_send()
-        return 0
-
-    lax.fori_loop(1, N, drain_raw, 0)
+        return 0
+
+    lax.fori_loop(1, N, arrive_raw, 0)
 
     def assemble(o, _):
         rows = pl.ds(pl.multiple_of(o * RAW * PART, RAW * PART), RAW * PART)
@@ -411,6 +415,17 @@
         return 0
 
     lax.fori_loop(0, N, assemble, 0)
+    attend_early(1, EARLY, raw_out, GROUP, COUNTS + 1)
+
+    def drain_near(d, _):
+        s = lax.rem(me + N - d, N)
+        q_copy(s, s).wait_send()
+        kv_copy(me, s, s).wait_send()
+        part_copy(s, s).wait_send()
+        raw_copy(s, s).wait_send()
+        return 0
+
+    lax.fori_loop(1, N, drain_near, 0)
 
     def drain_far(d, _):
         s = lax.rem(grp + N - d, N)
@@ -479,14 +494,11 @@
     lane = lax.broadcasted_iota(jnp.int32, (TILE, TILE), 1)
     clear_stages(buffers)
 
-    def first(r):
-        return jnp.minimum(tab[r, LISTED], EARLY)
-
     used, items = [], []
     for k in range(2):
         def gather(r, carry, base=k * HALF, k=k):
             n, total = carry
-            left = tab[r + base, LISTED + 1] - first(r + base)
+            left = tab[r + base, COUNTS + 2]
             rows[k, n] = r
             return n + jnp.where(left > 0, 1, 0), total + lax.div(left + CHUNK - 1, CHUNK)
 
@@ -499,7 +511,7 @@
         def fetch(r, c):
             row = jnp.minimum(r, HALF - 1) + base
             return jnp.concatenate(
-                [kv[tab[row, jnp.minimum(c + t, LISTED - 1)]] for t in range(CHUNK)], axis=0)
+                [kv[tab[row, jnp.minimum(c + t, LATE + LISTED - 1)]] for t in range(CHUNK)], axis=0)
         return fetch
 
     def advance(_, state):
@@ -511,20 +523,19 @@
                 pair_of = stream_buffers(buffers, k)
                 run_stages(
                     ((r0, c0), (r1, c1), (r2, c2), (r3, c3)), fetch_from(base),
-                    lambda row: tab[row, LISTED + 1], qz, base, states[k], pair_of[odd], pair_of[1 - odd])
+                    lambda row: LATE + tab[row, COUNTS + 2], qz, base, states[k], pair_of[odd], pair_of[1 - odd])
                 row = jnp.minimum(r0, HALF - 1) + base
-                more = (c0 + CHUNK < tab[row, LISTED + 1]) & (r0 < HALF)
+                more = (c0 + CHUNK < LATE + tab[row, COUNTS + 2]) & (r0 < HALF)
                 n = jnp.where(more, n, jnp.minimum(n + 1, used[k]))
                 rn = jnp.where(more, r0, rows[k, n])
-                cn = jnp.where(more, c0 + CHUNK, first(jnp.minimum(rn, HALF - 1) + base))
+                cn = jnp.where(more, c0 + CHUNK, LATE)
                 state[9 * k:9 * k + 9] = [n, rn, cn, r0, c0, r1, c1, r2, c2]
         return tuple(state)
 
-    zero, dummy = jnp.int32(0), jnp.int32(HALF)
+    zero, dummy, at = jnp.int32(0), jnp.int32(HALF), jnp.int32(LATE)
     start = []
     for k in range(2):
-        r = rows[k, 0]
-        start += [zero, r, first(jnp.minimum(r, HALF - 1) + k * HALF), dummy, zero, dummy, zero, dummy, zero]
+        start += [zero, rows[k, 0], at, dummy, at, dummy, at, dummy, at]
     lax.fori_loop(0, lax.div(jnp.maximum(items[0], items[1]) + 4, 2), advance, tuple(start))
 
     def close(acc, total, r):

time: 81 us -> 77.7 us (0.959)
  the two profiles are of different devices: /device:TPU:1 before, /device:TPU:8 now
where the time goes in v3:
time: 77.7 us; the launch traced here: 77.3 us
  Pallas kernels  76.4 us (98%)
  local copies, waits for them, and re-layouts  0.81 us (1%)
    pallas_call x1, Pallas kernels, exchange(): pl.pallas_call(exchange_kernel, out_shape=(jax.ShapeDtypeStruct((GROUP, T...  56.7 us
    pallas_call x1, Pallas kernels, finish(): pl.pallas_call(finish_kernel, out_shape=jax.ShapeDtypeStruct((2 * TILE, D...  11.7 us
    pallas_call x1, Pallas kernels, attend(): pl.pallas_call(attend_kernel, out_shape=(jax.ShapeDtypeStruct((N, TILE, T...  8.02 us

profile of v3, /device:TPU:8, one launch (start us, length us, event | category | flops | bytes accessed | tf_op | source)
XLA Modules:
  0.0 77.3 jit_solution(2919021220845774687)
XLA Ops:
  0.0 56.7 %exchange.1 = (bf16[32,128,128]{2,1,0:T(8,128)(2,1)S(1)}, bf16[32,128,128]{2,1,0:T(8,128)(2,1)S(1)}, bf16[32,128,128]{2,1,0:T(8,128)(2,1)S(1)}, bf16[32,128,128]...) custom-call(s32[32,512]{1,0:T(8,128)} %bitcast.4, ...), custom_call_target="tpu_custom_call" | custom-call | tf_op jit(solution)/shard_map/exchange/pallas_call | solution.py:445
  56.7 0.0 copy-start
  56.7 0.0 copy-start.1
  56.7 8.0 %attend.1 = (bf16[16,128,128]{2,1,0:T(8,128)(2,1)S(1)}, f32[17,128,128]{2,1,0:T(8,128)S(1)}, f32[17,128,128]{2,1,0:T(8,128)S(1)}, f32[17,128,128]{2,1,0:T(8,128)...) custom-call(s32[32,128]{1,0:T(8,128)S(1)} %get-tuple-element.17.tab,, ...), custom_call_target="tpu_custom_call", output_to_operand_aliasing={{1}: (5, {}), {2}: (6, {}), {3}: (7, {}), {4}: (8, {}), {5}... | custom-call | tf_op jit(solution)/shard_map/attend/pallas_call | solution.py:558
  64.8 0.0 copy-done
  64.8 0.0 copy-done.1
  64.8 11.7 %finish.1 = bf16[256,1024]{1,0:T(8,128)(2,1)S(1)} custom-call(bf16[16,128,128]{2,1,0:T(8,128)(2,1)S(1)} %get-tuple-element.28.att_ref, bf16[256,1024]{1,0:T(8,128)(2,1)S(1)} %copy-done, bf16[1024,1024]{1,0:T(8,128)(2,1)S(1)} %copy-done.1), custom_call_target="tpu_custom_call" | custom-call | tf_op jit(solution)/shard_map/finish/pallas_call | solution.py:619
  76.5 0.8 %copy.19 = bf16[256,1024]{1,0:T(8,128)(2,1)} copy(bf16[256,1024]{1,0:T(8,128)(2,1)S(1)} %finish.1) | data formatting | bytes 1048576
Async XLA Ops:
  56.7 8.1 %copy-start = (bf16[256,1024]{1,0:T(8,128)(2,1)S(1)}, bf16[256,1024]{1,0:T(8,128)(2,1)}, u32[]{:S(2)}) copy-start(bf16[256,1024]{1,0:T(8,128)(2,1)} %nodes_ref.1) | copy-start | bytes 1572868
  56.7 8.1 %copy-start.1 = (bf16[1024,1024]{1,0:T(8,128)(2,1)S(1)}, bf16[1024,1024]{1,0:T(8,128)(2,1)}, u32[]{:S(2)}) copy-start(bf16[1024,1024]{1,0:T(8,128)(2,1)} %w_ref.1) | copy-start | bytes 6291460

commit v4 on v3

--- a/solution.py
+++ b/solution.py
@@ -492,7 +492,6 @@
     kv[GROUP:GROUP + N * RAW] = raw_ref[...]
     kv[GROUP + N * RAW:] = far_ref[...]
     lane = lax.broadcasted_iota(jnp.int32, (TILE, TILE), 1)
-    clear_stages(buffers)
 
     used, items = [], []
     for k in range(2):
@@ -502,7 +501,7 @@
             rows[k, n] = r
             return n + jnp.where(left > 0, 1, 0), total + lax.div(left + CHUNK - 1, CHUNK)
 
-        n, total = lax.fori_loop(0, HALF, gather, (jnp.int32(0), jnp.int32(0)), unroll=4)
+        n, total = lax.fori_loop(0, HALF, gather, (jnp.int32(0), jnp.int32(0)), unroll=HALF)
         rows[k, n] = HALF
         used.append(n)
         items.append(total)
@@ -548,7 +547,7 @@
             out_ref[s + k * HALF // 2] = jnp.where(lane < HEAD_DIM, even, odd).astype(jnp.bfloat16)
         return 0
 
-    lax.fori_loop(0, HALF // 2, finish, 0)
+    lax.fori_loop(0, HALF // 2, finish, 0, unroll=2)
 
 
 def attend(tab, qz, kv, raw, far, *state):

time: 77.7 us -> 78.2 us (level)
    pallas_call x1, Pallas kernels: 11.7 us -> 12.6 us  [finish(): pl.pallas_call(finish_kernel, out_shape=jax.ShapeDtypeStruct((2 * TILE, D...]
where the time goes in v4:
time: 78.2 us; the launch traced here: 77.9 us
  Pallas kernels  77 us (98%)
  local copies, waits for them, and re-layouts  0.81 us (1%)
    pallas_call x1, Pallas kernels, exchange(): pl.pallas_call(exchange_kernel, out_shape=(jax.ShapeDtypeStruct((GROUP, T...  56.7 us
    pallas_call x1, Pallas kernels, finish(): pl.pallas_call(finish_kernel, out_shape=jax.ShapeDtypeStruct((2 * TILE, D...  12.6 us
    pallas_call x1, Pallas kernels, attend(): pl.pallas_call(attend_kernel, out_shape=(jax.ShapeDtypeStruct((N, TILE, T...  7.67 us

profile of v4, /device:TPU:8, one launch (start us, length us, event | category | flops | bytes accessed | tf_op | source)
XLA Modules:
  0.0 77.9 jit_solution(5782163863495781109)
XLA Ops:
  0.0 56.7 %exchange.1 = (bf16[32,128,128]{2,1,0:T(8,128)(2,1)S(1)}, bf16[32,128,128]{2,1,0:T(8,128)(2,1)S(1)}, bf16[32,128,128]{2,1,0:T(8,128)(2,1)S(1)}, bf16[32,128,128]...) custom-call(s32[32,512]{1,0:T(8,128)} %bitcast.4, ...), custom_call_target="tpu_custom_call" | custom-call | tf_op jit(solution)/shard_map/exchange/pallas_call | solution.py:445
  56.7 0.0 copy-start
  56.7 0.0 copy-start.1
  56.7 7.7 %attend.1 = (bf16[16,128,128]{2,1,0:T(8,128)(2,1)S(1)}, f32[17,128,128]{2,1,0:T(8,128)S(1)}, f32[17,128,128]{2,1,0:T(8,128)S(1)}, f32[17,128,128]{2,1,0:T(8,128)...) custom-call(s32[32,128]{1,0:T(8,128)S(1)} %get-tuple-element.17.tab,, ...), custom_call_target="tpu_custom_call", output_to_operand_aliasing={{1}: (5, {}), {2}: (6, {}), {3}: (7, {}), {4}: (8, {}), {5}... | custom-call | tf_op jit(solution)/shard_map/attend/pallas_call | solution.py:557
  64.4 0.0 copy-done
  64.4 0.0 copy-done.1
  64.4 12.6 %finish.1 = bf16[256,1024]{1,0:T(8,128)(2,1)S(1)} custom-call(bf16[16,128,128]{2,1,0:T(8,128)(2,1)S(1)} %get-tuple-element.28.att_ref, bf16[256,1024]{1,0:T(8,128)(2,1)S(1)} %copy-done, bf16[1024,1024]{1,0:T(8,128)(2,1)S(1)} %copy-done.1), custom_call_target="tpu_custom_call" | custom-call | tf_op jit(solution)/shard_map/finish/pallas_call | solution.py:618
  77.1 0.8 %copy.19 = bf16[256,1024]{1,0:T(8,128)(2,1)} copy(bf16[256,1024]{1,0:T(8,128)(2,1)S(1)} %finish.1) | data formatting | bytes 1048576
Async XLA Ops:
  56.7 7.7 %copy-start = (bf16[256,1024]{1,0:T(8,128)(2,1)S(1)}, bf16[256,1024]{1,0:T(8,128)(2,1)}, u32[]{:S(2)}) copy-start(bf16[256,1024]{1,0:T(8,128)(2,1)} %nodes_ref.1) | copy-start | bytes 1572868
  56.7 7.7 %copy-start.1 = (bf16[1024,1024]{1,0:T(8,128)(2,1)S(1)}, bf16[1024,1024]{1,0:T(8,128)(2,1)}, u32[]{:S(2)}) copy-start(bf16[1024,1024]{1,0:T(8,128)(2,1)} %w_ref.1) | copy-start | bytes 6291460
